TPU v7x, 32 devices: a whole 2x2x4 slice. The times are simulated.
32 devices in a mesh: ctx: 8 (over y, x, core), head: 4 (over z).
Axes of the slice: x: 2, y: 2, z: 4, core: 2. Of those that a mesh axis runs over, the one named last changes fastest.
Arguments:
- q_latent: bfloat16 [2048, 1536], P('ctx', 'head'), may hold values from -70 to 70
- kv_latent: bfloat16 [2048, 576], P('ctx', 'head'), may hold values from -6 to 6
- w_query: bfloat16 [1536, 12288], P(None, 'head'), may hold values from -0.15625 to 0.15625
- w_key: bfloat16 [512, 8192], P(None, 'head'), may hold values from -0.25 to 0.25
- w_value: bfloat16 [512, 8192], P(None, 'head'), may hold values from -0.25 to 0.25
- d_out: bfloat16 [2048, 8192], P('ctx', 'head'), may hold values from -6 to 6
Outputs:
- attn_out: bfloat16 [2048, 8192], P('ctx', 'head')
- grad_qlat: float32 [2048, 1536], P('ctx', 'head')
- grad_kvlat: float32 [2048, 576], P('ctx', 'head')
All inputs are finite; a program needn't handle non-finite values.
Results may differ from a plain program's by a relative error of at most 0.023.
The roundings to bfloat16 on the way count: a program that leaves them out, or rounds other values in their place, can miss the bound.
Values may be sent and summed in bfloat16 or wider, within the bound.
A program may use at most 128 MiB of HBM per device.

v0:
```python
import jax
import jax.numpy as jnp
from jax import lax
from jax.sharding import PartitionSpec as P

KVL = 512
ROPE = 64
NOPE = 128
VDIM = 128
HEAD_DEV = 16


def from_behind(array, axis, by):
    peers = lax.axis_size(axis)
    pairs = [(i, i + by) for i in range(peers) if 0 <= i + by < peers]
    return lax.ppermute(array, axis, pairs)


def on_device(q_latent, kv_latent, w_query, w_key, w_value, d_out):
    block_rows = q_latent.shape[0]
    per_dev = HEAD_DEV
    width = NOPE + ROPE
    softmax_scale = width ** (-0.5)
    queries = jnp.dot(
        lax.all_gather(q_latent, "head", axis=1, tiled=True),
        w_query,
        preferred_element_type=jnp.float32,
    )
    queries = queries.astype(jnp.bfloat16).reshape(block_rows, per_dev, width)
    latent = lax.all_gather(kv_latent, "head", axis=1, tiled=True)

    def expand(latent_rows):
        main_cols = latent_rows[:, :KVL]
        keys_nope = jnp.dot(main_cols, w_key, preferred_element_type=jnp.float32).astype(
            jnp.bfloat16
        )
        values = jnp.dot(main_cols, w_value, preferred_element_type=jnp.float32).astype(
            jnp.bfloat16
        )
        return (
            keys_nope.reshape(block_rows, per_dev, NOPE),
            latent_rows[:, KVL:],
            values.reshape(block_rows, per_dev, VDIM),
        )

    own_keys = expand(latent)
    previous = expand(from_behind(latent, "ctx", 1))
    keys_all = jnp.concatenate([previous[0], own_keys[0]], 0)
    rope_all = jnp.concatenate([previous[1], own_keys[1]], 0)
    values_all = jnp.concatenate([previous[2], own_keys[2]], 0)
    leading = lax.axis_index("ctx") == 0
    query_pos = jnp.arange(block_rows)[:, None]
    key_pos = jnp.arange(2 * block_rows)[None, :]
    visible = jnp.where(
        key_pos < block_rows, jnp.logical_not(leading), key_pos - block_rows <= query_pos
    )[None]
    query_nope = queries[..., :NOPE]
    query_rope = queries[..., NOPE:]
    scores = jnp.einsum("qhd,khd->hqk", query_nope, keys_all, preferred_element_type=jnp.float32)
    scores = (
        scores + jnp.einsum("qhr,kr->hqk", query_rope, rope_all, preferred_element_type=jnp.float32)
    ) * softmax_scale
    scores = jnp.where(visible, scores, jnp.float32(-1e30))
    maxima = jnp.max(scores, -1, keepdims=True)
    expons = jnp.where(visible, jnp.exp(scores - maxima), jnp.float32(0.0))
    probs = expons / jnp.sum(expons, -1, keepdims=True)
    probs_b = probs.astype(jnp.bfloat16)
    output = jnp.einsum(
        "hqk,khd->qhd", probs_b, values_all, preferred_element_type=jnp.float32
    ).astype(jnp.bfloat16)
    grad_out = d_out.reshape(block_rows, per_dev, VDIM)
    dprob = jnp.einsum("qhd,khd->hqk", grad_out, values_all, preferred_element_type=jnp.float32)
    row_dot = jnp.sum(grad_out.astype(jnp.float32) * output.astype(jnp.float32), -1).T[..., None]
    dscore = (probs * (dprob - row_dot) * softmax_scale).astype(jnp.bfloat16)
    grad_qnope = jnp.einsum("hqk,khd->qhd", dscore, keys_all, preferred_element_type=jnp.float32)
    grad_qrope = jnp.einsum("hqk,kr->qhr", dscore, rope_all, preferred_element_type=jnp.float32)
    grad_query = (
        jnp.concatenate([grad_qnope, grad_qrope], -1)
        .astype(jnp.bfloat16)
        .reshape(block_rows, per_dev * width)
    )
    grad_qpart = jnp.dot(grad_query, w_query.T, preferred_element_type=jnp.float32)
    grad_knope = jnp.einsum(
        "hqk,qhd->khd", dscore, query_nope, preferred_element_type=jnp.float32
    ).astype(jnp.bfloat16)
    grad_krope = jnp.einsum(
        "hqk,qhr->khr", dscore, query_rope, preferred_element_type=jnp.float32
    ).astype(jnp.bfloat16)
    grad_value = jnp.einsum(
        "hqk,qhd->khd", probs_b, grad_out, preferred_element_type=jnp.float32
    ).astype(jnp.bfloat16)

    def project(knope_part, krope_part, value_part):
        main_cols = jnp.dot(
            knope_part.reshape(block_rows, per_dev * NOPE),
            w_key.T,
            preferred_element_type=jnp.float32,
        )
        main_cols = main_cols + jnp.dot(
            value_part.reshape(block_rows, per_dev * VDIM),
            w_value.T,
            preferred_element_type=jnp.float32,
        )
        rope_cols = jnp.sum(krope_part.astype(jnp.float32), axis=1)
        return jnp.concatenate([main_cols, rope_cols], -1)

    own_part = project(grad_knope[block_rows:], grad_krope[block_rows:], grad_value[block_rows:])
    earlier = project(grad_knope[:block_rows], grad_krope[:block_rows], grad_value[:block_rows])
    grad_kvpart = own_part + from_behind(earlier.astype(jnp.bfloat16), "ctx", -1).astype(
        earlier.dtype
    )
    grad_qlat, grad_kvlat = (
        lax.psum_scatter(grad_qpart, "head", scatter_dimension=1, tiled=True),
        lax.psum_scatter(grad_kvpart, "head", scatter_dimension=1, tiled=True),
    )
    return (output.reshape(block_rows, per_dev * VDIM), grad_qlat, grad_kvlat)


def solution(mesh):
    return jax.shard_map(
        on_device,
        mesh=mesh,
        in_specs=(
            P("ctx", "head"),
            P("ctx", "head"),
            P(None, "head"),
            P(None, "head"),
            P(None, "head"),
            P("ctx", "head"),
        ),
        out_specs=(P("ctx", "head"), P("ctx", "head"), P("ctx", "head")),
        check_vma=False,
    )
```

profile of v0, /device:TPU:0, one launch (start us, length us, event | category | flops | bytes accessed | tf_op | source)
XLA Modules:
  0.0 189.1 jit_solution(5349100622864666267)
XLA Ops:
  7.2 16.0 %all_gather.6 = bf16[256,576]{0,1:T(8,128)(2,1)S(1)} all-gather(bf16[256,144]{0,1:T(8,128)(2,1)} %param.7), channel_id=1, replica_groups=mesh['ctx'=8,'head'=4] {'head'}, dimensions={1}, use_global_device_ids=true | all-gather | bytes 368640 | tf_op jit(solution)/shard_map/all_gather | solution.py:30
  23.2 2.0 %collective-permute-start = (bf16[256,576]{0,1:T(8,128)(2,1)S(1)}, bf16[256,576]{0,1:T(8,128)(2,1)}, u32[]{:S(2)}, u32[]{:S(2)}) collective-permute-start(bf16[256,576]{0,1:T(8,128)(2,1)S(1)} %all_gather.6), channel_id=1, source_target_pairs={{0,4},{4,8},{8,12},{12,16},{16,20},{20,24},{24,28},{1,5},{5,9},{9,... | collective-permute-start | bytes 884744 | tf_op jit(solution)/shard_map/ppermute | solution.py:16
  25.3 20.2 %all_gather.7 = bf16[256,1536]{1,0:T(8,128)(2,1)S(1)} all-gather(bf16[256,384]{1,0:T(8,128)(2,1)} %param.6), channel_id=1, replica_groups=mesh['ctx'=8,'head'=4] {'head'}, dimensions={1}, use_global_device_ids=true | all-gather | bytes 983040 | tf_op jit(solution)/shard_map/all_gather | solution.py:25
  45.5 3.3 %convolution_convert_fusion.3 = bf16[256,2048]{1,0:T(8,128)(2,1)} fusion(bf16[512,2048]{1,0:T(8,128)(2,1)} %param.10, bf16[256,576]{0,1:T(8,128)(2,1)S(1)} %all_gather.6), kind=kOutput, calls=%fused_computation.13 | convolution fusion | flops 537395200 | bytes 3407872 | tf_op jit(solution)/shard_map/dot_general | solution.py:37
  48.7 7.4 %convolution_convert_fusion = bf16[256,3072]{1,0:T(8,128)(2,1)} fusion(bf16[256,1536]{1,0:T(8,128)(2,1)S(1)} %all_gather.7, bf16[1536,3072]{1,0:T(8,128)(2,1)} %param.8), kind=kOutput, calls=%fused_computation.9 | convolution fusion | flops 2416705536 | bytes 11796480 | tf_op jit(solution)/shard_map/dot_general | solution.py:24
  56.9 2.6 %copy.41 = bf16[256,3072]{0,1:T(8,128)(2,1)} copy(bf16[256,3072]{1,0:T(8,128)(2,1)} %convolution_convert_fusion) | data formatting | bytes 3145728 | tf_op jit(solution)/shard_map/convert_element_type | solution.py:29
  59.5 1.5 copy.46
  61.0 2.3 %copy.63 = bf16[256,2048]{0,1:T(8,128)(2,1)} copy(bf16[256,2048]{1,0:T(8,128)(2,1)} %convolution_convert_fusion.3) | data formatting | bytes 2097152 | tf_op jit(solution)/shard_map/reshape | solution.py:43
  63.3 1.7 fusion.7
  65.0 2.7 %convolution_convert_fusion.4 = bf16[256,2048]{1,0:T(8,128)(2,1)} fusion(bf16[512,2048]{1,0:T(8,128)(2,1)S(1)} %copy-done.2, bf16[256,576]{0,1:T(8,128)(2,1)} %collective-permute-done), kind=kOutput, calls=%fused_computation.14 | convolution fusion | flops 537395200 | bytes 3407872 | tf_op jit(solution)/shard_map/dot_general | solution.py:37
  67.6 2.3 %copy.62 = bf16[256,2048]{0,1:T(8,128)(2,1)} copy(bf16[256,2048]{1,0:T(8,128)(2,1)} %convolution_convert_fusion.4) | data formatting | bytes 2097152 | tf_op jit(solution)/shard_map/reshape | solution.py:43
  69.9 1.8 fusion.6
  73.1 4.5 %fusion.12 = f32[16,256,512]{2,1,0:T(8,128)} fusion(bf16[512,16,128]{2,0,1:T(8,128)(2,1)S(1)} %bitcast_dynamic-update-slice_fusion, bf16[256,16,192]{0,2,1:T(8,128)(2,1)S(1)} %bitcast.82), kind=kOutput, calls=%fused_computation.35 | convolution fusion | flops 536870912 | bytes 11534336 | tf_op jit(solution)/shard_map/qhd,khd->hqk/dot_general | solution.py:59
  78.4 10.6 %fusion.28 = (f32[16,256]{1,0:T(8,128)S(1)}, f32[16,256,512]{2,1,0:T(8,128)}) fusion(pred[256,512]{1,0:T(8,128)(4,1)S(1)} %copy-done.14, f32[16,256,512]{2,1,0:T(8,128)} %fusion.12, bf16[256,16,192]{0,2,1:T(8,128)(2,1)} %bitcast.81, bf16[256,64]{0,1:T(8,128)(2,1)S(1)} %slice.52, bf16[256,64]{0,1:T(8,128)(2,1)S(1)} %slice.51), kind=kOutput, calls=%fused_computation.58 | convolution fusion | flops 281149952 | bytes 17645568 | tf_op jit(solution)/shard_map/sub | solution.py:65
  89.0 3.9 %fusion.5 = bf16[16,256,512]{2,1,0:T(8,128)(2,1)S(1)} fusion(f32[16,256,512]{2,1,0:T(8,128)} %get-tuple-element.17, f32[16,256]{1,0:T(8,128)S(1)} %get-tuple-element.16), kind=kLoop, calls=%fused_computation.10 | loop fusion | flops 4194304 | bytes 12599296 | tf_op jit(solution)/shard_map/convert_element_type | solution.py:67
  94.5 2.5 %multiply_reduce_fusion = (f32[256,16]{0,1:T(8,128)S(1)}, bf16[16,128,256]{2,1,0:T(8,128)(2,1)}) fusion(bf16[256,2048]{0,1:T(8,128)(2,1)S(1)} %copy.46, bf16[16,256,512]{2,1,0:T(8,128)(2,1)S(1)} %fusion.5, bf16[256,16,128]{0,2,1:T(8,128)(2,1)S(1)} %bitcast.93, bf16[256,16,128]{0,2,1:T(8,128)(2,1)S(1)} %bitcast.95), kind=kOutput, calls=%fused_computation.18 | convolution fusion | flops 543682560 | bytes 8404992 | tf_op jit(solution)/shard_map/hqk,khd->qhd/dot_general | solution.py:68
  97.2 2.3 %fusion.2 = bf16[16,256,512]{2,1,0:T(8,128)(2,1)S(1)} fusion(f32[16,256]{1,0:T(8,128)S(1)} %bitcast.101, f32[16,256,512]{2,1,0:T(8,128)S(1)} %bitcast.86, f32[16,256]{1,0:T(8,128)S(1)} %get-tuple-element.16, bf16[256,16,128]{0,2,1:T(8,128)(2,1)S(1)} %bitcast.88, bf16[256,16,128]{0,2,1:T(8,128)(2,1)S(1)} %bitcast.94, bf16[256,16,128]{0,2,1:T(8,128)(2,1)S(1)} %bitcast.96), kind=kOutput, calls=%fused_computation.3 | convolution fusion | flops 551550976 | bytes 15761408 | tf_op jit(solution)/shard_map/qhd,khd->hqk/dot_general | solution.py:72
  99.5 1.5 fusion.8
  101.1 1.0 copy-done.7
  103.8 1.6 fusion.26
  105.7 1.6 fusion.33
  107.3 1.6 fusion.32
  109.1 2.9 %fusion.11 = bf16[256,512]{1,0:T(8,128)(2,1)S(1)} fusion(f32[256,512]{1,0:T(8,128)} %fusion.33, bf16[256,2048]{0,1:T(8,128)(2,1)} %bitcast.97, bf16[512,2048]{1,0:T(8,128)(2,1)} %param.10), kind=kOutput, calls=%fused_computation.31 | convolution fusion | flops 537133056 | bytes 3932160 | tf_op jit(solution)/shard_map/dot_general | solution.py:99
  112.0 1.3 collective-permute-start.1
  114.1 1.4 collective-permute-done.1
  116.5 2.1 %copy.64 = f32[256,576]{0,1:T(8,128)} copy(f32[256,576]{1,0:T(8,128)} %maximum_add_fusion) | data formatting | bytes 1179648
  118.7 3.6 %fusion.10 = bf16[256,16,64]{0,2,1:T(8,128)(2,1)S(1)} fusion(bf16[16,256,512]{2,1,0:T(8,128)(2,1)} %copy-done.1, bf16[256,64]{0,1:T(8,128)(2,1)S(1)} %slice.52, bf16[256,64]{0,1:T(8,128)(2,1)S(1)} %slice.51), kind=kOutput, calls=%fused_computation.28 | convolution fusion | flops 268828672 | bytes 4784128 | tf_op jit(solution)/shard_map/hqk,kr->qhr/dot_general | solution.py:76
  122.4 7.6 %fusion.31 = f32[256,1536]{1,0:T(8,128)} fusion(bf16[256,3072]{0,1:T(8,128)(2,1)S(1)} %bitcast.91, bf16[1536,3072]{1,0:T(8,128)(2,1)} %param.8), kind=kOutput, calls=%fused_computation.59 | convolution fusion | flops 2415919104 | bytes 12582912 | tf_op jit(solution)/shard_map/dot_general | solution.py:82
  130.0 1.2 copy-done.10
  131.2 1.4 copy.54
  132.6 13.0 %reduce-scatter.7.cloned.1.call-done = f32[144,256]{1,0:T(8,128)} async-done(((f32[576,256]{1,0:T(8,128)}), f32[144,256]{1,0:T(8,128)}) %reduce-scatter.7.cloned.1.call-update) | async-done | bytes 147472
  145.6 36.7 %reduce-scatter.5.cloned.1.call-done = f32[256,384]{1,0:T(8,128)} async-done(((f32[256,1536]{1,0:T(8,128)}), f32[256,384]{1,0:T(8,128)}) %reduce-scatter.5.cloned.1.call-update) | async-done | bytes 393232 | tf_op jit(solution)/shard_map/reduce_scatter | solution.py:113
  (57 shorter events, 8.8 us)
Async XLA Ops:
  7.2 56.1 %copy-start = (bf16[512,2048]{1,0:T(8,128)(2,1)S(1)}, bf16[512,2048]{1,0:T(8,128)(2,1)}, u32[]{:S(2)}) copy-start(bf16[512,2048]{1,0:T(8,128)(2,1)} %param.9) | copy-start | bytes 6291460
  7.2 138.4 %reduce-scatter.7.cloned.1.call-start = ((), (), s32[]{:S(2)}) async-start(), calls=%async_computation.3 | async-start | bytes 737280
  23.2 41.7 %collective-permute-start = (bf16[256,576]{0,1:T(8,128)(2,1)S(1)}, bf16[256,576]{0,1:T(8,128)(2,1)}, u32[]{:S(2)}, u32[]{:S(2)}) collective-permute-start(bf16[256,576]{0,1:T(8,128)(2,1)S(1)} %all_gather.6), channel_id=1, source_target_pairs={{0,4},{4,8},{8,12},{12,16},{16,20},{20,24},{24,28},{1,5},{5,9},{9,... | collective-permute-start | bytes 884744 | tf_op jit(solution)/shard_map/ppermute | solution.py:16
  63.3 1.7 copy-start.2
  69.9 2.1 %copy-start.8 = (bf16[32,16,8,128]{3,2,1,0:T(8,128)(2,1)S(1)}, bf16[32,16,8,128]{3,2,1,0:T(8,128)(2,1)}, u32[]{:S(2)}) copy-start(bf16[32,16,8,128]{3,2,1,0:T(8,128)(2,1)} %fusion.7) | copy-start | bytes 3145732
  71.7 1.4 copy-start.6
  72.3 5.3 %copy-start.4 = (bf16[512,16,128]{2,0,1:T(8,128)(2,1)}, bf16[512,16,128]{2,0,1:T(8,128)(2,1)S(1)}, u32[]{:S(2)}) copy-start(bf16[512,16,128]{2,0,1:T(8,128)(2,1)S(1)} %bitcast_dynamic-update-slice_fusion) | copy-start | bytes 6291460
  73.1 5.3 %copy-start.14 = (pred[256,512]{1,0:T(8,128)(4,1)S(1)}, pred[256,512]{1,0:T(8,128)(4,1)}, u32[]{:S(2)}) copy-start(pred[256,512]{1,0:T(8,128)(4,1)} %fusion.15) | copy-start | bytes 393220
  92.9 1.2 copy-start.11
  92.9 1.5 copy-start.12
  92.9 4.0 %slice-start = ((s8[8388608]{0:T(1024)(128)(4,1)}), s8[4194304]{0:T(1024)(128)(4,1)S(1)}, s32[]{:S(2)}) async-start(s8[8388608]{0:T(1024)(128)(4,1)} %bitcast.85), calls=%async_computation.4 | async-start | bytes 8388608
  94.5 2.7 %slice-start.1 = ((s8[8388608]{0:T(1024)(128)(4,1)}), s8[4194304]{0:T(1024)(128)(4,1)S(1)}, s32[]{:S(2)}) async-start(s8[8388608]{0:T(1024)(128)(4,1)} %bitcast.85), calls=%async_computation.5 | async-start | bytes 8388608
  97.2 2.3 %copy-start.5 = (bf16[512,16,128]{2,0,1:T(8,128)(2,1)S(1)}, bf16[512,16,128]{2,0,1:T(8,128)(2,1)}, u32[]{:S(2)}) copy-start(bf16[512,16,128]{2,0,1:T(8,128)(2,1)} %copy-done.4) | copy-start | bytes 6291460
  99.5 3.4 %copy-start.1 = (bf16[16,256,512]{2,1,0:T(8,128)(2,1)}, bf16[16,256,512]{2,1,0:T(8,128)(2,1)S(1)}, u32[]{:S(2)}) copy-start(bf16[16,256,512]{2,1,0:T(8,128)(2,1)S(1)} %fusion.2) | copy-start | bytes 12582916
  99.5 2.6 %copy-start.7 = (bf16[256,3072]{0,1:T(8,128)(2,1)S(1)}, bf16[256,3072]{0,1:T(8,128)(2,1)}, u32[]{:S(2)}) copy-start(bf16[256,3072]{0,1:T(8,128)(2,1)} %copy.41) | copy-start | bytes 4718596
  109.1 4.3 %copy-start.3 = (bf16[512,2048]{1,0:T(8,128)(2,1)S(1)}, bf16[512,2048]{1,0:T(8,128)(2,1)}, u32[]{:S(2)}) copy-start(bf16[512,2048]{1,0:T(8,128)(2,1)} %param.10) | copy-start | bytes 6291460
  109.1 4.3 %copy-start.9 = (bf16[256,16,128]{0,2,1:T(8,128)(2,1)S(1)}, bf16[256,16,128]{0,2,1:T(8,128)(2,1)}, u32[]{:S(2)}) copy-start(bf16[256,16,128]{0,2,1:T(8,128)(2,1)} %get-tuple-element.13) | copy-start | bytes 3145732
  109.1 4.3 %copy-start.13 = (f32[256,512]{1,0:T(8,128)S(1)}, f32[256,512]{1,0:T(8,128)}, u32[]{:S(2)}) copy-start(f32[256,512]{1,0:T(8,128)} %fusion.32) | copy-start | bytes 1572868
  112.0 3.5 %collective-permute-start.1 = (bf16[256,576]{1,0:T(8,128)(2,1)S(1)}, bf16[256,576]{1,0:T(8,128)(2,1)S(1)}, u32[]{:S(2)}, u32[]{:S(2)}) collective-permute-start(bf16[256,576]{1,0:T(8,128)(2,1)S(1)} %pad_maximum_fusion.4), channel_id=1, source_target_pairs={{4,0},{8,4},{12,8},{16,12},{20,16},{24,20},{28,24},{5,1},{9,5},{13... | collective-permute-start | bytes 884744 | tf_op jit(solution)/shard_map/ppermute | solution.py:16
  118.6 63.6 %reduce-scatter.5.cloned.1.call-start = ((), (), s32[]{:S(2)}) async-start(), calls=%async_computation.2 | async-start | bytes 1966080 | tf_op jit(solution)/shard_map/reduce_scatter | solution.py:113
  129.9 1.2 copy-start.10
Sparse Core Ops, SparseCore 0:
  118.8 26.7 reduce-scatter.6
  148.4 33.7 reduce-scatter.4
where the time goes:
time: 190 us; the launch traced here: 189 us
  matrix products  58.5 us (31%)
  waiting for transfers between devices  51.1 us (27%)
  blocking collectives  36.2 us (19%)
  local copies, waits for them, and re-layouts  19.7 us (10%)
  between operations  14.3 us (8%)
  other arithmetic  5.84 us (3%)
  starting transfers between devices  3.38 us (2%)
    reduce_scatter x1, waiting for transfers between devices, on_device(): lax.psum_scatter(grad_qpart, 'head', scatter_dimension=1, tiled=True)  36.7 us
    all_gather x1, blocking collectives, on_device(): lax.all_gather(q_latent, 'head', axis=1, tiled=True)  20.2 us
    all_gather x1, blocking collectives, on_device(): latent = lax.all_gather(kv_latent, 'head', axis=1, tiled=True)  16 us
    unnamed x3, waiting for transfers between devices  13 us
    sub x1, matrix products, on_device(): expons = jnp.where(visible, jnp.exp(scores - maxima), jnp.float32(0.0))  10.6 us
    unnamed x38, local copies, waits for them, and re-layouts  9.38 us
    dot_general x1, matrix products, on_device(): jnp.dot(grad_query, w_query.T, preferred_element_type=jnp.float32)  7.55 us
    dot_general x1, matrix products, on_device(): jnp.dot(lax.all_gather(q_latent, 'head', axis=1, tiled=True), w_query, pr...  7.4 us
  transfers between devices with their start and end apart: 4, of which 3 were waited for; matrix products, arithmetic and copies ran while one was open for 17% of the time, Pallas kernels for 0%

commit v1 on v0

--- a/solution.py
+++ b/solution.py
@@ -22,7 +22,9 @@
     width = NOPE + ROPE
     softmax_scale = width ** (-0.5)
     queries = jnp.dot(
-        lax.all_gather(q_latent, "head", axis=1, tiled=True),
+        jnp.concatenate(
+            lax.all_to_all(jnp.stack([q_latent] * lax.axis_size("head")), "head", 0, 0), axis=1
+        ),
         w_query,
         preferred_element_type=jnp.float32,
     )

time: 190 us -> 183 us (0.963)
  blocking collectives: 36.2 us -> 16 us
  starting transfers between devices: 3.38 us -> 8 us
  matrix products: 58.5 us -> 61.9 us
  waiting for transfers between devices: 51.1 us -> 54.4 us
  local copies, waits for them, and re-layouts: 19.7 us -> 21.9 us
    all_gather x1 -> x0, blocking collectives: 20.2 us -> none  [on_device(): lax.all_gather(q_latent, 'head', axis=1, tiled=True)]
    all_to_all x0 -> x1, starting transfers between devices: none -> 5.37 us  [on_device(): lax.all_to_all(jnp.stack([q_latent] * lax.axis_size('head')), 'head', 0, 0)]
    dot_general x1, matrix products: 1.51 us -> 4.64 us  [on_device(): jnp.einsum('hqk,khd->qhd', dscore, keys_all, preferred_element_type=jnp.f...]
    all_to_all x0 -> x1, waiting for transfers between devices: none -> 2.92 us  [on_device(): lax.all_to_all(jnp.stack([q_latent] * lax.axis_size('head')), 'head', 0, 0)]
    dot_general x1, matrix products: 4.54 us -> 6.48 us  [on_device(): jnp.einsum('qhd,khd->hqk', query_nope, keys_all, preferred_element_type=j...]
    unnamed x38 -> x35, local copies, waits for them, and re-layouts: 9.38 us -> 10.5 us
  transfers between devices with their start and end apart: 4 -> 5, of which waited for: 3 -> 4; matrix products, arithmetic and copies ran while one was open for 17% -> 18% of each run, Pallas kernels for 0% -> 0%
where the time goes in v1:
time: 183 us; the launch traced here: 182 us
  matrix products  61.9 us (34%)
  waiting for transfers between devices  54.4 us (30%)
  local copies, waits for them, and re-layouts  21.9 us (12%)
  blocking collectives  16 us (9%)
  between operations  14.3 us (8%)
  starting transfers between devices  8 us (4%)
  other arithmetic  5.92 us (3%)
    reduce_scatter x1, waiting for transfers between devices, on_device(): lax.psum_scatter(grad_qpart, 'head', scatter_dimension=1, tiled=True)  36.7 us
    all_gather x1, blocking collectives, on_device(): latent = lax.all_gather(kv_latent, 'head', axis=1, tiled=True)  16 us
    unnamed x3, waiting for transfers between devices  13.1 us
    sub x1, matrix products, on_device(): expons = jnp.where(visible, jnp.exp(scores - maxima), jnp.float32(0.0))  10.6 us
    unnamed x35, local copies, waits for them, and re-layouts  10.5 us
    dot_general x1, matrix products, on_device(): jnp.dot(grad_query, w_query.T, preferred_element_type=jnp.float32)  7.55 us
    dot_general x1, matrix products, on_device(): jnp.dot(jnp.concatenate(lax.all_to_all(jnp.stack([q_latent] * lax.axis_si...  7.47 us
    dot_general x1, matrix products, on_device(): jnp.einsum('qhd,khd->hqk', query_nope, keys_all, preferred_element_type=j...  6.48 us
  transfers between devices with their start and end apart: 5, of which 4 were waited for; matrix products, arithmetic and copies ran while one was open for 18% of the time, Pallas kernels for 0%

profile of v1, /device:TPU:0, one launch (start us, length us, event | category | flops | bytes accessed | tf_op | source)
XLA Modules:
  0.0 182.4 jit_solution(9700368672400016256)
XLA Ops:
  7.2 16.0 %all_gather.3 = bf16[256,576]{0,1:T(8,128)(2,1)S(1)} all-gather(bf16[256,144]{0,1:T(8,128)(2,1)} %param.7), channel_id=1, replica_groups=mesh['ctx'=8,'head'=4] {'head'}, dimensions={1}, use_global_device_ids=true | all-gather | bytes 368640 | tf_op jit(solution)/shard_map/all_gather | solution.py:32
  23.2 1.3 collective-permute-start
  26.6 5.4 %all-to-all-start = ((bf16[4,256,384]{1,2,0:T(8,128)(2,1)}), bf16[4,256,384]{1,2,0:T(8,128)(2,1)S(1)}, u32[]{:S(2)}, u32[]{:S(2)}) async-start(bf16[4,256,384]{1,2,0:T(8,128)(2,1)} %stack.2), calls=%async_computation | async-start | bytes 1572864 | tf_op jit(solution)/shard_map/all_to_all | solution.py:26
  32.0 1.7 fusion.7
  33.7 1.7 convolution_convert_fusion.3
  36.1 2.3 %copy.48 = bf16[256,2048]{0,1:T(8,128)(2,1)} copy(bf16[256,2048]{1,0:T(8,128)(2,1)} %param.11) | data formatting | bytes 2097152 | tf_op args[5]
  38.4 2.3 %copy.65 = bf16[256,2048]{0,1:T(8,128)(2,1)} copy(bf16[256,2048]{1,0:T(8,128)(2,1)} %convolution_convert_fusion.3) | data formatting | bytes 2097152 | tf_op jit(solution)/shard_map/reshape | solution.py:45
  40.7 3.3 %convolution_convert_fusion.4 = bf16[256,2048]{1,0:T(8,128)(2,1)} fusion(bf16[512,2048]{1,0:T(8,128)(2,1)} %param.10, bf16[256,576]{0,1:T(8,128)(2,1)S(1)} %collective-permute-done), kind=kOutput, calls=%fused_computation.14 | convolution fusion | flops 537395200 | bytes 3407872 | tf_op jit(solution)/shard_map/dot_general | solution.py:39
  44.0 2.3 %copy.64 = bf16[256,2048]{0,1:T(8,128)(2,1)} copy(bf16[256,2048]{1,0:T(8,128)(2,1)} %convolution_convert_fusion.4) | data formatting | bytes 2097152 | tf_op jit(solution)/shard_map/reshape | solution.py:45
  47.0 1.3 bitcast_dynamic-update-slice_fusion.1
  48.3 1.3 bitcast_dynamic-update-slice_fusion
  49.6 2.9 %all-to-all-done = bf16[4,256,384]{1,2,0:T(8,128)(2,1)S(1)} async-done(((bf16[4,256,384]{1,2,0:T(8,128)(2,1)}), bf16[4,256,384]{1,2,0:T(8,128)(2,1)S(1)}, u32[]{:S(2)}, u32[]{:S(2)}) %all-to-all-start) | async-done | bytes 786464 | tf_op jit(solution)/shard_map/all_to_all | solution.py:26
  52.5 7.5 %convolution_convert_fusion = bf16[256,3072]{1,0:T(8,128)(2,1)} fusion(bf16[256,1536]{0,1:T(8,128)(2,1)S(1)} %bitcast.90, bf16[1536,3072]{1,0:T(8,128)(2,1)} %param.8), kind=kOutput, calls=%fused_computation.9 | convolution fusion | flops 2416705536 | bytes 11796480 | tf_op jit(solution)/shard_map/dot_general | solution.py:24
  60.0 2.6 %copy.43 = bf16[256,3072]{0,1:T(8,128)(2,1)} copy(bf16[256,3072]{1,0:T(8,128)(2,1)} %convolution_convert_fusion) | data formatting | bytes 3145728 | tf_op jit(solution)/shard_map/convert_element_type | solution.py:31
  62.6 6.5 %fusion.12 = f32[16,256,512]{2,1,0:T(8,128)} fusion(bf16[512,16,128]{2,0,1:T(8,128)(2,1)} %bitcast_dynamic-update-slice_fusion, bf16[256,16,192]{0,2,1:T(8,128)(2,1)} %bitcast.84), kind=kOutput, calls=%fused_computation.35 | convolution fusion | flops 536870912 | bytes 11534336 | tf_op jit(solution)/shard_map/qhd,khd->hqk/dot_general | solution.py:61
  69.0 10.6 %fusion.28 = (f32[16,256]{1,0:T(8,128)S(1)}, f32[16,256,512]{2,1,0:T(8,128)}) fusion(pred[256,512]{1,0:T(8,128)(4,1)S(1)} %copy-done.12, f32[16,256,512]{2,1,0:T(8,128)} %fusion.12, bf16[256,16,192]{0,2,1:T(8,128)(2,1)} %bitcast.85, bf16[256,64]{0,1:T(8,128)(2,1)S(1)} %slice.52, bf16[256,64]{0,1:T(8,128)(2,1)S(1)} %slice.51), kind=kOutput, calls=%fused_computation.58 | convolution fusion | flops 281149952 | bytes 17645568 | tf_op jit(solution)/shard_map/sub | solution.py:67
  79.7 3.9 %fusion.5 = bf16[16,256,512]{2,1,0:T(8,128)(2,1)S(1)} fusion(f32[16,256,512]{2,1,0:T(8,128)} %get-tuple-element.17, f32[16,256]{1,0:T(8,128)S(1)} %get-tuple-element.16), kind=kLoop, calls=%fused_computation.10 | loop fusion | flops 4194304 | bytes 12599296 | tf_op jit(solution)/shard_map/convert_element_type | solution.py:69
  85.2 2.5 %multiply_reduce_fusion = (f32[256,16]{0,1:T(8,128)S(1)}, bf16[16,128,256]{2,1,0:T(8,128)(2,1)}) fusion(bf16[256,2048]{0,1:T(8,128)(2,1)S(1)} %copy-done.5, bf16[16,256,512]{2,1,0:T(8,128)(2,1)S(1)} %fusion.5, bf16[256,16,128]{0,2,1:T(8,128)(2,1)S(1)} %bitcast.97, bf16[256,16,128]{0,2,1:T(8,128)(2,1)S(1)} %bitcast.99), kind=kOutput, calls=%fused_computation.18 | convolution fusion | flops 543682560 | bytes 8404992 | tf_op jit(solution)/shard_map/hqk,khd->qhd/dot_general | solution.py:70
  87.9 2.5 %fusion.2 = bf16[16,256,512]{2,1,0:T(8,128)(2,1)S(1)} fusion(f32[16,256]{1,0:T(8,128)S(1)} %bitcast.105, f32[16,256,512]{2,1,0:T(8,128)S(1)} %bitcast.89, f32[16,256]{1,0:T(8,128)S(1)} %get-tuple-element.16, bf16[256,16,128]{0,2,1:T(8,128)(2,1)S(1)} %bitcast.92, bf16[256,16,128]{0,2,1:T(8,128)(2,1)S(1)} %bitcast.98, bf16[256,16,128]{0,2,1:T(8,128)(2,1)S(1)} %bitcast.100), kind=kOutput, calls=%fused_computation.3 | convolution fusion | flops 551550976 | bytes 15761408 | tf_op jit(solution)/shard_map/qhd,khd->hqk/dot_general | solution.py:74
  90.4 4.6 %fusion.8 = bf16[256,16,128]{0,2,1:T(8,128)(2,1)S(1)} fusion(bf16[512,16,128]{2,0,1:T(8,128)(2,1)} %bitcast_dynamic-update-slice_fusion, bf16[16,256,512]{2,1,0:T(8,128)(2,1)S(1)} %fusion.2), kind=kOutput, calls=%fused_computation.25 | convolution fusion | flops 537395200 | bytes 7340032 | tf_op jit(solution)/shard_map/hqk,khd->qhd/dot_general | solution.py:77
  96.8 1.6 fusion.26
  98.7 1.6 fusion.33
  100.3 1.6 fusion.32
  102.1 2.9 %fusion.11 = bf16[256,512]{1,0:T(8,128)(2,1)S(1)} fusion(f32[256,512]{1,0:T(8,128)} %fusion.33, bf16[256,2048]{0,1:T(8,128)(2,1)} %bitcast.101, bf16[512,2048]{1,0:T(8,128)(2,1)} %param.10), kind=kOutput, calls=%fused_computation.31 | convolution fusion | flops 537133056 | bytes 3932160 | tf_op jit(solution)/shard_map/dot_general | solution.py:101
  105.0 1.3 collective-permute-start.1
  107.1 1.7 collective-permute-done.1
  109.8 2.1 %copy.66 = f32[256,576]{0,1:T(8,128)} copy(f32[256,576]{1,0:T(8,128)} %maximum_add_fusion) | data formatting | bytes 1179648
  112.0 3.6 %fusion.10 = bf16[256,16,64]{0,2,1:T(8,128)(2,1)S(1)} fusion(bf16[16,256,512]{2,1,0:T(8,128)(2,1)} %copy-done.1, bf16[256,64]{0,1:T(8,128)(2,1)S(1)} %slice.52, bf16[256,64]{0,1:T(8,128)(2,1)S(1)} %slice.51), kind=kOutput, calls=%fused_computation.28 | convolution fusion | flops 268828672 | bytes 4784128 | tf_op jit(solution)/shard_map/hqk,kr->qhr/dot_general | solution.py:78
  115.6 7.5 %fusion.31 = f32[256,1536]{1,0:T(8,128)} fusion(bf16[256,3072]{0,1:T(8,128)(2,1)S(1)} %bitcast.95, bf16[1536,3072]{1,0:T(8,128)(2,1)} %param.8), kind=kOutput, calls=%fused_computation.59 | convolution fusion | flops 2415919104 | bytes 12582912 | tf_op jit(solution)/shard_map/dot_general | solution.py:84
  124.4 1.4 copy.56
  125.8 13.1 %reduce-scatter.7.cloned.1.call-done = f32[144,256]{1,0:T(8,128)} async-done(((f32[576,256]{1,0:T(8,128)}), f32[144,256]{1,0:T(8,128)}) %reduce-scatter.7.cloned.1.call-update) | async-done | bytes 147472
  138.9 36.7 %reduce-scatter.5.cloned.1.call-done = f32[256,384]{1,0:T(8,128)} async-done(((f32[256,1536]{1,0:T(8,128)}), f32[256,384]{1,0:T(8,128)}) %reduce-scatter.5.cloned.1.call-update) | async-done | bytes 393232 | tf_op jit(solution)/shard_map/reduce_scatter | solution.py:115
  (56 shorter events, 10.7 us)
Async XLA Ops:
  7.2 24.8 %copy-start = (bf16[512,2048]{1,0:T(8,128)(2,1)S(1)}, bf16[512,2048]{1,0:T(8,128)(2,1)}, u32[]{:S(2)}) copy-start(bf16[512,2048]{1,0:T(8,128)(2,1)} %param.9) | copy-start | bytes 6291460
  23.2 17.5 %collective-permute-start = (bf16[256,576]{0,1:T(8,128)(2,1)S(1)}, bf16[256,576]{0,1:T(8,128)(2,1)S(1)}, u32[]{:S(2)}, u32[]{:S(2)}) collective-permute-start(bf16[256,576]{0,1:T(8,128)(2,1)S(1)} %all_gather.3), channel_id=1, source_target_pairs={{0,4},{4,8},{8,12},{12,16},{16,20},{20,24},{24,28},{1,5},{5,9},{9,... | collective-permute-start | bytes 884744 | tf_op jit(solution)/shard_map/ppermute | solution.py:16
  26.6 25.9 %all-to-all-start = ((bf16[4,256,384]{1,2,0:T(8,128)(2,1)}), bf16[4,256,384]{1,2,0:T(8,128)(2,1)S(1)}, u32[]{:S(2)}, u32[]{:S(2)}) async-start(bf16[4,256,384]{1,2,0:T(8,128)(2,1)} %stack.2), calls=%async_computation | async-start | bytes 1572864 | tf_op jit(solution)/shard_map/all_to_all | solution.py:26
  31.9 107.0 %reduce-scatter.7.cloned.1.call-start = ((), (), s32[]{:S(2)}) async-start(), calls=%async_computation.4 | async-start | bytes 737280
  31.9 1.7 copy-start.2
  46.3 2.1 %copy-start.6 = (bf16[32,16,8,128]{3,2,1,0:T(8,128)(2,1)S(1)}, bf16[32,16,8,128]{3,2,1,0:T(8,128)(2,1)}, u32[]{:S(2)}) copy-start(bf16[32,16,8,128]{3,2,1,0:T(8,128)(2,1)} %fusion.7) | copy-start | bytes 3145732
  62.6 6.5 %copy-start.12 = (pred[256,512]{1,0:T(8,128)(4,1)S(1)}, pred[256,512]{1,0:T(8,128)(4,1)}, u32[]{:S(2)}) copy-start(pred[256,512]{1,0:T(8,128)(4,1)} %fusion.15) | copy-start | bytes 393220
  79.7 3.9 %copy-start.5 = (bf16[256,2048]{0,1:T(8,128)(2,1)S(1)}, bf16[256,2048]{0,1:T(8,128)(2,1)}, u32[]{:S(2)}) copy-start(bf16[256,2048]{0,1:T(8,128)(2,1)} %copy.48) | copy-start | bytes 3145732
  83.6 1.2 copy-start.9
  83.6 1.5 copy-start.10
  83.6 4.0 %slice-start = ((s8[8388608]{0:T(1024)(128)(4,1)}), s8[4194304]{0:T(1024)(128)(4,1)S(1)}, s32[]{:S(2)}) async-start(s8[8388608]{0:T(1024)(128)(4,1)} %bitcast.88), calls=%async_computation.5 | async-start | bytes 8388608
  85.2 2.7 %slice-start.1 = ((s8[8388608]{0:T(1024)(128)(4,1)}), s8[4194304]{0:T(1024)(128)(4,1)S(1)}, s32[]{:S(2)}) async-start(s8[8388608]{0:T(1024)(128)(4,1)} %bitcast.88), calls=%async_computation.6 | async-start | bytes 8388608
  90.4 5.5 %copy-start.1 = (bf16[16,256,512]{2,1,0:T(8,128)(2,1)}, bf16[16,256,512]{2,1,0:T(8,128)(2,1)S(1)}, u32[]{:S(2)}) copy-start(bf16[16,256,512]{2,1,0:T(8,128)(2,1)S(1)} %fusion.2) | copy-start | bytes 12582916
  90.4 4.7 %copy-start.4 = (bf16[256,3072]{0,1:T(8,128)(2,1)S(1)}, bf16[256,3072]{0,1:T(8,128)(2,1)}, u32[]{:S(2)}) copy-start(bf16[256,3072]{0,1:T(8,128)(2,1)} %copy.43) | copy-start | bytes 4718596
  102.1 4.3 %copy-start.3 = (bf16[512,2048]{1,0:T(8,128)(2,1)S(1)}, bf16[512,2048]{1,0:T(8,128)(2,1)}, u32[]{:S(2)}) copy-start(bf16[512,2048]{1,0:T(8,128)(2,1)} %param.10) | copy-start | bytes 6291460
  102.1 4.3 %copy-start.7 = (bf16[256,16,128]{0,2,1:T(8,128)(2,1)S(1)}, bf16[256,16,128]{0,2,1:T(8,128)(2,1)}, u32[]{:S(2)}) copy-start(bf16[256,16,128]{0,2,1:T(8,128)(2,1)} %get-tuple-element.13) | copy-start | bytes 3145732
  102.1 4.3 %copy-start.11 = (f32[256,512]{1,0:T(8,128)S(1)}, f32[256,512]{1,0:T(8,128)}, u32[]{:S(2)}) copy-start(f32[256,512]{1,0:T(8,128)} %fusion.32) | copy-start | bytes 1572868
  105.0 3.8 %collective-permute-start.1 = (bf16[256,576]{1,0:T(8,128)(2,1)S(1)}, bf16[256,576]{1,0:T(8,128)(2,1)S(1)}, u32[]{:S(2)}, u32[]{:S(2)}) collective-permute-start(bf16[256,576]{1,0:T(8,128)(2,1)S(1)} %pad_maximum_fusion.4), channel_id=1, source_target_pairs={{4,0},{8,4},{12,8},{16,12},{20,16},{24,20},{28,24},{5,1},{9,5},{13... | collective-permute-start | bytes 884744 | tf_op jit(solution)/shard_map/ppermute | solution.py:16
  111.9 63.6 %reduce-scatter.5.cloned.1.call-start = ((), (), s32[]{:S(2)}) async-start(), calls=%async_computation.3 | async-start | bytes 1966080 | tf_op jit(solution)/shard_map/reduce_scatter | solution.py:115
  123.2 1.2 copy-start.8
Sparse Core Ops, SparseCore 0:
  112.0 26.8 reduce-scatter.6
  141.8 33.7 reduce-scatter.4
